TPU v7x, 32 devices: a whole 2x2x4 slice. The times are simulated.
32 devices in a mesh: row: 8 (over z, y), col: 4 (over x, core).
Axes of the slice: x: 2, y: 2, z: 4, core: 2. Of those that a mesh axis runs over, the one named last changes fastest.
Arguments:
- embeddings: bfloat16 [12288, 768], P(('row', 'col'))
- doc_order: int32 [12288], P(('row', 'col')), may hold values from 0 to 12287, each once
Outputs:
- nearest_earlier: float32 [12288], P(('row', 'col'))
Inputs may be any that keep to these rules, and one draw needn't show every extreme that they name: `doc_order`: each value 0 to 12287 appears once.
All inputs are finite; a program needn't handle non-finite values.
Results may differ from a plain program's by a relative error of at most 0.00051.
Values may be sent and summed in bfloat16 or wider, within the bound.
No kernel may reach another device: no remote copies, remote signals or barrier semaphores. Data moves between devices by JAX's collectives and lax.ppermute only.
A program may use at most 64 MiB of HBM per device.

v0:
```python
import jax
import jax.numpy as jnp
from jax import lax
from jax.sharding import PartitionSpec as P


def normalize_rows(embeddings):
    floats = embeddings.astype(jnp.float32)
    scale = lax.rsqrt(jnp.sum(floats * floats, axis=1, keepdims=True) + 1e-06)
    return (floats * scale).astype(jnp.bfloat16)


def block_size(length):
    width = min(512, length)
    while length % width != 0:
        width = width - 1
    return width


def masked_maxima(row_units, row_orders, col_units, col_orders, running):
    length = col_units.shape[0]
    width = block_size(length)
    col_groups = col_units.reshape(length // width, width, col_units.shape[1])
    order_groups = col_orders.reshape(length // width, width)

    def one_block(current, pair):
        units_here, orders_here = pair
        scores = jnp.dot(row_units, units_here.T, preferred_element_type=jnp.float32)
        earlier = orders_here[None, :] < row_orders[:, None]
        masked = jnp.where(earlier, scores, jnp.float32(-1.0))
        return (jnp.maximum(current, jnp.max(masked, axis=1)), None)

    result, unused = lax.scan(one_block, running, (col_groups, order_groups))
    return result


def shards(embeddings, doc_order):
    unit_rows = normalize_rows(embeddings)
    own_rows = unit_rows.shape[0]
    col_count = lax.axis_size("col")
    block_rows = own_rows * col_count
    initial = jnp.full((block_rows,), -1.0, jnp.float32)
    row_units, row_orders = (
        lax.all_gather(unit_rows, "col", axis=0, tiled=True),
        lax.all_gather(doc_order, "col", axis=0, tiled=True),
    )
    best_rows = masked_maxima(
        row_units,
        row_orders,
        lax.all_gather(unit_rows, "row", axis=0, tiled=True),
        lax.all_gather(doc_order, "row", axis=0, tiled=True),
        initial,
    )
    whole_max = lax.pmax(best_rows, "col")
    own_share = lax.dynamic_slice_in_dim(whole_max, lax.axis_index("col") * own_rows, own_rows, 0)
    return jnp.maximum(own_share, jnp.float32(-1.0))


def solution(mesh):
    return jax.shard_map(
        shards,
        mesh=mesh,
        in_specs=(P(("row", "col"), None), P(("row", "col"))),
        out_specs=P(("row", "col")),
        check_vma=False,
    )
```

profile of v0, /device:TPU:0, one launch (start us, length us, event | category | flops | bytes accessed | tf_op | source)
XLA Modules:
  0.0 152.0 jit_solution(297163370144080767)
XLA Ops:
  6.5 0.0 copy-start
  6.5 0.0 all-gather.7.cloned.1.call-start
  6.5 1.3 fusion.5
  7.8 2.0 %fusion.6 = bf16[384,768]{1,0:T(8,128)(2,1)} fusion(bf16[384,768]{1,0:T(8,128)(2,1)} %param.4, f32[384]{0:T(512)S(1)} %add_rsqrt_fusion), kind=kLoop, calls=%fused_computation.11 | loop fusion | flops 884736 | bytes 1181184 | tf_op jit(solution)/shard_map/convert_element_type | solution.py:10
  9.9 0.0 all-gather.7.cloned.1.call-update
  9.9 0.0 all-gather.5.cloned.1.call-start
  9.9 0.7 all-gather.5.cloned.1.call-update
  10.7 0.0 copy-done
  10.7 27.8 %all-gather = s32[8,1,384]{2,1,0:T(1,128)S(1)} all-gather(s32[1,1,384]{2,1,0:T(1,128)S(1)} %reshape.15), channel_id=1, replica_groups=mesh['row'=8,'col'=4] {'row'}, dimensions={0}, use_global_device_ids=true | all-gather | bytes 13824 | tf_op jit(solution)/shard_map/all_gather | solution.py:51
  38.6 5.2 %all-gather.1 = s32[4,1,384]{2,1,0:T(1,128)S(1)} all-gather(s32[1,1,384]{2,1,0:T(1,128)S(1)} %reshape.15), channel_id=1, replica_groups=mesh['row'=8,'col'=4] {'col'}, dimensions={0}, use_global_device_ids=true | all-gather | bytes 7680 | tf_op jit(solution)/shard_map/all_gather | solution.py:45
  43.8 0.0 all-gather.7.cloned.1.call-done
  43.8 74.5 %all-gather.5.cloned.1.call-done = bf16[3072,768]{1,0:T(8,128)(2,1)} async-done(((bf16[384,768]{1,0:T(8,128)(2,1)}), bf16[3072,768]{1,0:T(8,128)(2,1)}) %all-gather.5.cloned.1.call-update) | async-done | bytes 4718608 | tf_op jit(solution)/shard_map/all_gather | solution.py:50
  118.3 20.4 %while.11 = (s32[]{:T(128)}, f32[1536]{0:T(1024)S(1)}, s32[6,512]{1,0:T(8,128)S(1)}, s32[1536]{0:T(1024)S(1)}, bf16[6,512,768]{2,1,0:T(8,128)(2,1)}, /*index=5*/bf16[1536,768]{1,0:T(8,128)(2,1)}, s32[]{:T(128)}, s32[]{:T(128)}) while((s32[]{:T(128)}, f32[1536]{0:T(1024)S(1)}, s32[6,512]{1,0:T(8,128)S(1)}, s32[1536]{0:T(1024)S(1)}, ...), condition=%wide.region_3.4_spmd.clone, body=%wide.region_1.3_spmd.clone.sunk | while | flops 1210320384 | bytes 3183203 | solution.py:33
  118.4 3.3 %fusion.13 = f32[1536]{0:T(1024)S(1)} fusion(bf16[1536,768]{1,0:T(8,128)(2,1)} %get-tuple-element.129, s32[1536]{0:T(1024)S(1)} %get-tuple-element.127, s32[512]{0:T(512)S(1)} %bitcast.20, bf16[6,512,768]{2,1,0:T(8,128)(2,1)} %get-tuple-element.128, s32[]{:T(128)} %get-tuple-element.116), kind=kOutput, calls=%fused_computation.2.clone.1 | convolution fusion | flops 1210317312 | bytes 3160576 | tf_op jit(solution)/shard_map/while/body/eval_jaxpr/dot_general | solution.py:28
  121.8 3.3 %fusion.13 = f32[1536]{0:T(1024)S(1)} fusion(bf16[1536,768]{1,0:T(8,128)(2,1)} %get-tuple-element.129, s32[1536]{0:T(1024)S(1)} %get-tuple-element.127, s32[512]{0:T(512)S(1)} %bitcast.20, bf16[6,512,768]{2,1,0:T(8,128)(2,1)} %get-tuple-element.128, s32[]{:T(128)} %get-tuple-element.116), kind=kOutput, calls=%fused_computation.2.clone.1 | convolution fusion | flops 1210317312 | bytes 3160576 | tf_op jit(solution)/shard_map/while/body/eval_jaxpr/dot_general | solution.py:28
  125.2 3.3 %fusion.13 = f32[1536]{0:T(1024)S(1)} fusion(bf16[1536,768]{1,0:T(8,128)(2,1)} %get-tuple-element.129, s32[1536]{0:T(1024)S(1)} %get-tuple-element.127, s32[512]{0:T(512)S(1)} %bitcast.20, bf16[6,512,768]{2,1,0:T(8,128)(2,1)} %get-tuple-element.128, s32[]{:T(128)} %get-tuple-element.116), kind=kOutput, calls=%fused_computation.2.clone.1 | convolution fusion | flops 1210317312 | bytes 3160576 | tf_op jit(solution)/shard_map/while/body/eval_jaxpr/dot_general | solution.py:28
  128.6 3.3 %fusion.13 = f32[1536]{0:T(1024)S(1)} fusion(bf16[1536,768]{1,0:T(8,128)(2,1)} %get-tuple-element.129, s32[1536]{0:T(1024)S(1)} %get-tuple-element.127, s32[512]{0:T(512)S(1)} %bitcast.20, bf16[6,512,768]{2,1,0:T(8,128)(2,1)} %get-tuple-element.128, s32[]{:T(128)} %get-tuple-element.116), kind=kOutput, calls=%fused_computation.2.clone.1 | convolution fusion | flops 1210317312 | bytes 3160576 | tf_op jit(solution)/shard_map/while/body/eval_jaxpr/dot_general | solution.py:28
  132.0 3.3 %fusion.13 = f32[1536]{0:T(1024)S(1)} fusion(bf16[1536,768]{1,0:T(8,128)(2,1)} %get-tuple-element.129, s32[1536]{0:T(1024)S(1)} %get-tuple-element.127, s32[512]{0:T(512)S(1)} %bitcast.20, bf16[6,512,768]{2,1,0:T(8,128)(2,1)} %get-tuple-element.128, s32[]{:T(128)} %get-tuple-element.116), kind=kOutput, calls=%fused_computation.2.clone.1 | convolution fusion | flops 1210317312 | bytes 3160576 | tf_op jit(solution)/shard_map/while/body/eval_jaxpr/dot_general | solution.py:28
  135.4 3.3 %fusion.13 = f32[1536]{0:T(1024)S(1)} fusion(bf16[1536,768]{1,0:T(8,128)(2,1)} %get-tuple-element.129, s32[1536]{0:T(1024)S(1)} %get-tuple-element.127, s32[512]{0:T(512)S(1)} %bitcast.20, bf16[6,512,768]{2,1,0:T(8,128)(2,1)} %get-tuple-element.128, s32[]{:T(128)} %get-tuple-element.116), kind=kOutput, calls=%fused_computation.2.clone.1 | convolution fusion | flops 1210317312 | bytes 3160576 | tf_op jit(solution)/shard_map/while/body/eval_jaxpr/dot_general | solution.py:28
  138.7 5.8 %pmax.7 = f32[1536]{0:T(1024)S(1)} all-reduce(f32[1536]{0:T(1024)S(1)} %get-tuple-element.37), channel_id=1, replica_groups=mesh['row'=8,'col'=4] {'col'}, use_global_device_ids=true, to_apply=%region_4.5 | all-reduce | flops 1536 | bytes 12288 | tf_op jit(solution)/shard_map/pmax | solution.py:54
  144.5 0.7 dynamic-slice_maximum_fusion
  (19 shorter events, 0.2 us)
Async XLA Ops:
  6.5 4.1 %copy-start = (s32[384]{0:T(512)S(1)}, s32[384]{0:T(512)}, u32[]{:S(2)}) copy-start(s32[384]{0:T(512)} %param.5) | copy-start | bytes 4612
  6.5 37.3 %all-gather.7.cloned.1.call-start = ((), (), s32[]{:S(2)}) async-start(), calls=%async_computation.1 | async-start | bytes 2949120 | tf_op jit(solution)/shard_map/all_gather | solution.py:44
  9.9 108.5 %all-gather.5.cloned.1.call-start = ((), (), s32[]{:S(2)}) async-start(), calls=%async_computation | async-start | bytes 5308416 | tf_op jit(solution)/shard_map/all_gather | solution.py:50
Sparse Core Ops, SparseCore 0:
  10.0 26.7 all-gather.6
  39.0 79.3 all-gather.4
where the time goes:
time: 152 us
  waiting for transfers between devices  75.3 us (50%)
  blocking collectives  38.8 us (26%)
  matrix products  20.1 us (13%)
  between operations  13.5 us (9%)
  other arithmetic  4.08 us (3%)
    all_gather x1, waiting for transfers between devices, shards(): lax.all_gather(unit_rows, 'row', axis=0, tiled=True)  74.5 us
    all_gather x1, blocking collectives, shards(): lax.all_gather(doc_order, 'row', axis=0, tiled=True)  27.8 us
    dot_general x6, matrix products, one_block(): jnp.dot(row_units, units_here.T, preferred_element_type=jnp.float32)  20.1 us
    pmax x1, blocking collectives, shards(): whole_max = lax.pmax(best_rows, 'col')  5.77 us
    all_gather x1, blocking collectives, shards(): lax.all_gather(doc_order, 'col', axis=0, tiled=True)  5.18 us
  transfers between devices with their start and end apart: 2, of which 1 were waited for; matrix products, arithmetic and copies ran while one was open for 0% of the time, Pallas kernels for 0%

commit v1 on v0

--- a/solution.py
+++ b/solution.py
@@ -2,6 +2,28 @@
 import jax.numpy as jnp
 from jax import lax
 from jax.sharding import PartitionSpec as P
+
+
+def joined_along(pieces, dim):
+    pieces = jnp.moveaxis(pieces, 0, dim)
+    shape = pieces.shape
+    return pieces.reshape(*shape[:dim], shape[dim] * shape[dim + 1], *shape[dim + 2 :])
+
+
+def ring_gather(array, axis, dim):
+    size = lax.axis_size(axis)
+    pairs = [(i, (i + 1) % size) for i in range(size)]
+    back = [(b, a) for a, b in pairs]
+    lower, upper = ([], [])
+    for step in range(size - 1):
+        if step % 2 == 0:
+            lower.append(lax.ppermute(lower[-1] if lower else array, axis, pairs))
+        else:
+            upper.append(lax.ppermute(upper[-1] if upper else array, axis, back))
+    blocks = jnp.stack([*lower[::-1], array, *upper])
+    shift = lax.axis_index(axis) - len(lower)
+    blocks = blocks[(jnp.arange(size) - shift) % size]
+    return joined_along(blocks, dim)
 
 
 def normalize_rows(embeddings):
@@ -47,7 +69,7 @@
     best_rows = masked_maxima(
         row_units,
         row_orders,
-        lax.all_gather(unit_rows, "row", axis=0, tiled=True),
+        ring_gather(unit_rows, "row", 0),
         lax.all_gather(doc_order, "row", axis=0, tiled=True),
         initial,
     )

time: 152 us -> 188 us (1.24)
  starting transfers between devices: 0.04 us -> 29.3 us
  waiting for transfers between devices: 75.3 us -> 52.7 us
  local copies, waits for them, and re-layouts: 0.07 us -> 19.5 us
  blocking collectives: 38.8 us -> 45.8 us
  other arithmetic: 4.08 us -> 6.32 us
    all_gather x1 -> x0, waiting for transfers between devices: 74.5 us -> none  [shards(): lax.all_gather(unit_rows, 'row', axis=0, tiled=True)]
    ppermute x0 -> x7, waiting for transfers between devices: none -> 52.6 us  [the longest x4 46.8 us: ring_gather(): lower.append(lax.ppermute(lower[-1] if lower else array, axis, pairs))]
    ppermute x0 -> x7, starting transfers between devices: none -> 29.3 us  [the longest x3 21.3 us: ring_gather(): upper.append(lax.ppermute(upper[-1] if upper else array, axis, back))]
    unnamed x4 -> x18, local copies, waits for them, and re-layouts: 0.02 us -> 7.61 us
    all_gather x1, blocking collectives: 27.8 us -> 33.9 us  [shards(): lax.all_gather(doc_order, 'row', axis=0, tiled=True)]
    gather x0 -> x1, local copies, waits for them, and re-layouts: none -> 5.31 us  [ring_gather(): blocks = blocks[(jnp.arange(size) - shift) % size]]
    dynamic_slice x6, local copies, waits for them, and re-layouts: 0.05 us -> 4.36 us  [masked_maxima(): result, unused = lax.scan(one_block, running, (col_groups, order_groups))]
  transfers between devices with their start and end apart: 2 -> 8, of which waited for: 1 -> 4; matrix products, arithmetic and copies ran while one was open for 0% -> 10% of each run, Pallas kernels for 0% -> 0%
where the time goes in v1:
time: 188 us; the launch traced here: 187 us
  waiting for transfers between devices  52.7 us (28%)
  blocking collectives  45.8 us (24%)
  starting transfers between devices  29.3 us (16%)
  matrix products  20 us (11%)
  local copies, waits for them, and re-layouts  19.5 us (10%)
  between operations  13.5 us (7%)
  other arithmetic  6.32 us (3%)
    ppermute x4, waiting for transfers between devices, ring_gather(): lower.append(lax.ppermute(lower[-1] if lower else array, axis, pairs))  46.8 us
    all_gather x1, blocking collectives, shards(): lax.all_gather(doc_order, 'row', axis=0, tiled=True)  33.9 us
    ppermute x3, starting transfers between devices, ring_gather(): upper.append(lax.ppermute(upper[-1] if upper else array, axis, back))  21.3 us
    dot_general x6, matrix products, one_block(): jnp.dot(row_units, units_here.T, preferred_element_type=jnp.float32)  20 us
    ppermute x4, starting transfers between devices, ring_gather(): lower.append(lax.ppermute(lower[-1] if lower else array, axis, pairs))  8.01 us
    unnamed x18, local copies, waits for them, and re-layouts  7.61 us
    pmax x1, blocking collectives, shards(): whole_max = lax.pmax(best_rows, 'col')  6.36 us
    ppermute x3, waiting for transfers between devices, ring_gather(): upper.append(lax.ppermute(upper[-1] if upper else array, axis, back))  5.82 us
  transfers between devices with their start and end apart: 8, of which 4 were waited for; matrix products, arithmetic and copies ran while one was open for 10% of the time, Pallas kernels for 0%

profile of v1, /device:TPU:0, one launch (start us, length us, event | category | flops | bytes accessed | tf_op | source)
XLA Modules:
  0.0 187.3 jit_solution(13195945414176586034)
XLA Ops:
  6.5 1.3 fusion.5
  7.9 1.2 fusion.6
  9.1 3.0 %collective-permute-start = (bf16[384,768]{1,0:T(8,128)(2,1)S(1)}, bf16[384,768]{1,0:T(8,128)(2,1)S(1)}, u32[]{:S(2)}, u32[]{:S(2)}) collective-permute-start(bf16[384,768]{1,0:T(8,128)(2,1)S(1)} %fusion.6), channel_id=1, source_target_pairs={{0,4},{4,8},{8,12},{12,16},{16,20},{20,24},{24,28},{28,0},{1,5},{5... | collective-permute-start | bytes 1769480 | tf_op jit(solution)/shard_map/ppermute | solution.py:20
  12.2 16.4 %collective-permute-done = bf16[384,768]{1,0:T(8,128)(2,1)S(1)} collective-permute-done((bf16[384,768]{1,0:T(8,128)(2,1)S(1)}, bf16[384,768]{1,0:T(8,128)(2,1)S(1)}, u32[]{:S(2)}, u32[]{:S(2)}) %collective-permute-start) | collective-permute-done | bytes 589856 | tf_op jit(solution)/shard_map/ppermute | solution.py:20
  28.6 4.8 %collective-permute-start.4 = (bf16[384,768]{1,0:T(8,128)(2,1)}, bf16[384,768]{1,0:T(8,128)(2,1)S(1)}, u32[]{:S(2)}, u32[]{:S(2)}) collective-permute-start(bf16[384,768]{1,0:T(8,128)(2,1)} %copy-done.1), channel_id=1, source_target_pairs={{4,0},{8,4},{12,8},{16,12},{20,16},{24,20},{28,24},{0,28},{5,1},{9... | collective-permute-start | bytes 1769480 | tf_op jit(solution)/shard_map/ppermute | solution.py:22
  33.3 20.1 %collective-permute-done.1 = bf16[384,768]{1,0:T(8,128)(2,1)S(1)} collective-permute-done((bf16[384,768]{1,0:T(8,128)(2,1)S(1)}, bf16[384,768]{1,0:T(8,128)(2,1)S(1)}, u32[]{:S(2)}, u32[]{:S(2)}) %collective-permute-start.1) | collective-permute-done | bytes 589856 | tf_op jit(solution)/shard_map/ppermute | solution.py:20
  53.5 2.5 %collective-permute-start.2 = (bf16[384,768]{1,0:T(8,128)(2,1)S(1)}, bf16[384,768]{1,0:T(8,128)(2,1)S(1)}, u32[]{:S(2)}, u32[]{:S(2)}) collective-permute-start(bf16[384,768]{1,0:T(8,128)(2,1)S(1)} %collective-permute-done.1), channel_id=1, source_target_pairs={{0,4},{4,8},{8,12},{12,16},{16,20},{20,24},{24,28},{28,0},{1,5},{5... | collective-permute-start | bytes 1769480 | tf_op jit(solution)/shard_map/ppermute | solution.py:20
  56.0 13.7 %collective-permute-start.5 = (bf16[384,768]{1,0:T(8,128)(2,1)S(1)}, bf16[384,768]{1,0:T(8,128)(2,1)S(1)}, u32[]{:S(2)}, u32[]{:S(2)}) collective-permute-start(bf16[384,768]{1,0:T(8,128)(2,1)S(1)} %collective-permute-done.4), channel_id=1, source_target_pairs={{4,0},{8,4},{12,8},{16,12},{20,16},{24,20},{28,24},{0,28},{5,1},{9... | collective-permute-start | bytes 1769480 | tf_op jit(solution)/shard_map/ppermute | solution.py:22
  69.7 10.3 %collective-permute-done.2 = bf16[384,768]{1,0:T(8,128)(2,1)S(1)} collective-permute-done((bf16[384,768]{1,0:T(8,128)(2,1)S(1)}, bf16[384,768]{1,0:T(8,128)(2,1)S(1)}, u32[]{:S(2)}, u32[]{:S(2)}) %collective-permute-start.2) | collective-permute-done | bytes 589856 | tf_op jit(solution)/shard_map/ppermute | solution.py:20
  80.0 2.5 %collective-permute-start.3 = (bf16[384,768]{1,0:T(8,128)(2,1)S(1)}, bf16[384,768]{1,0:T(8,128)(2,1)}, u32[]{:S(2)}, u32[]{:S(2)}) collective-permute-start(bf16[384,768]{1,0:T(8,128)(2,1)S(1)} %collective-permute-done.2), channel_id=1, source_target_pairs={{0,4},{4,8},{8,12},{12,16},{16,20},{20,24},{24,28},{28,0},{1,5},{5... | collective-permute-start | bytes 1769480 | tf_op jit(solution)/shard_map/ppermute | solution.py:20
  83.2 33.9 %all-gather = s32[8,1,384]{2,1,0:T(1,128)} all-gather(s32[1,1,384]{2,1,0:T(1,128)S(1)} %reshape.68), channel_id=1, replica_groups=mesh['row'=8,'col'=4] {'row'}, dimensions={0}, use_global_device_ids=true | all-gather | bytes 13824 | tf_op jit(solution)/shard_map/all_gather | solution.py:73
  117.1 1.3 reduce
  118.4 1.3 reshape.59
  119.7 5.6 %all-gather.1 = s32[4,1,384]{2,1,0:T(1,128)} all-gather(s32[1,1,384]{2,1,0:T(1,128)S(1)} %reshape.68), channel_id=1, replica_groups=mesh['row'=8,'col'=4] {'col'}, dimensions={0}, use_global_device_ids=true | all-gather | bytes 7680 | tf_op jit(solution)/shard_map/all_gather | solution.py:67
  126.7 2.8 %collective-permute-start.6 = (bf16[384,768]{1,0:T(8,128)(2,1)S(1)}, bf16[384,768]{1,0:T(8,128)(2,1)S(1)}, u32[]{:S(2)}, u32[]{:S(2)}) collective-permute-start(bf16[384,768]{1,0:T(8,128)(2,1)S(1)} %collective-permute-done.5), channel_id=1, source_target_pairs={{4,0},{8,4},{12,8},{16,12},{20,16},{24,20},{28,24},{0,28},{5,1},{9... | collective-permute-start | bytes 1769480 | tf_op jit(solution)/shard_map/ppermute | solution.py:22
  129.5 1.9 %bitcast_dynamic-update-slice_fusion.7 = bf16[8,384,768]{2,1,0:T(8,128)(2,1)} fusion(bf16[384,768]{1,0:T(8,128)(2,1)} %collective-permute-done.3), kind=kLoop, calls=%fused_computation.20 | loop fusion | bytes 1179648
  131.4 0.9 bitcast_dynamic-update-slice_fusion.6
  132.3 0.9 bitcast_dynamic-update-slice_fusion.5
  133.1 0.9 bitcast_dynamic-update-slice_fusion.4
  134.0 1.0 bitcast_dynamic-update-slice_fusion.3
  135.8 0.9 bitcast_dynamic-update-slice_fusion.1
  136.8 5.8 %collective-permute-done.6 = bf16[384,768]{1,0:T(8,128)(2,1)S(1)} collective-permute-done((bf16[384,768]{1,0:T(8,128)(2,1)S(1)}, bf16[384,768]{1,0:T(8,128)(2,1)S(1)}, u32[]{:S(2)}, u32[]{:S(2)}) %collective-permute-start.6) | collective-permute-done | bytes 589856 | tf_op jit(solution)/shard_map/ppermute | solution.py:22
  142.6 0.9 bitcast_dynamic-update-slice_fusion
  143.5 5.3 %gather_fusion = bf16[8,384,768]{2,1,0:T(8,128)(2,1)} fusion(bf16[8,384,768]{2,1,0:T(8,128)(2,1)} %bitcast_dynamic-update-slice_fusion, s32[1024]{0:T(1024)S(1)} %pad_clamp_fusion), kind=kCustom, calls=%fused_computation | custom fusion | bytes 9437216 | tf_op jit(solution)/shard_map/gather | solution.py:25
  148.8 24.6 %while.11 = (s32[]{:T(128)}, f32[1536]{0:T(1024)S(1)}, s32[6,512]{1,0:T(8,128)}, s32[1536]{0:T(1024)S(1)}, bf16[6,512,768]{2,1,0:T(8,128)(2,1)}, /*index=5*/bf16[1536,768]{1,0:T(8,128)(2,1)}, s32[]{:T(128)}, s32[]{:T(128)}) while((s32[]{:T(128)}, f32[1536]{0:T(1024)S(1)}, s32[6,512]{1,0:T(8,128)}, s32[1536]{0:T(1024)S(1)}, ...), condition=%wide.region_3.4_spmd.clone, body=%wide.region_1.3_spmd.clone.sunk | while | flops 1210320384 | bytes 3183203 | solution.py:55
  149.5 3.3 %fusion.15 = f32[1536]{0:T(1024)S(1)} fusion(bf16[1536,768]{1,0:T(8,128)(2,1)} %get-tuple-element.129, s32[1536]{0:T(1024)S(1)} %get-tuple-element.127, s32[512]{0:T(512)S(1)} %bitcast.39, bf16[6,512,768]{2,1,0:T(8,128)(2,1)} %get-tuple-element.128, s32[]{:T(128)} %get-tuple-element.116), kind=kOutput, calls=%fused_computation.3.clone.1 | convolution fusion | flops 1210317312 | bytes 3160576 | tf_op jit(solution)/shard_map/while/body/eval_jaxpr/dot_general | solution.py:50
  153.7 3.3 %fusion.15 = f32[1536]{0:T(1024)S(1)} fusion(bf16[1536,768]{1,0:T(8,128)(2,1)} %get-tuple-element.129, s32[1536]{0:T(1024)S(1)} %get-tuple-element.127, s32[512]{0:T(512)S(1)} %bitcast.39, bf16[6,512,768]{2,1,0:T(8,128)(2,1)} %get-tuple-element.128, s32[]{:T(128)} %get-tuple-element.116), kind=kOutput, calls=%fused_computation.3.clone.1 | convolution fusion | flops 1210317312 | bytes 3160576 | tf_op jit(solution)/shard_map/while/body/eval_jaxpr/dot_general | solution.py:50
  157.8 3.3 %fusion.15 = f32[1536]{0:T(1024)S(1)} fusion(bf16[1536,768]{1,0:T(8,128)(2,1)} %get-tuple-element.129, s32[1536]{0:T(1024)S(1)} %get-tuple-element.127, s32[512]{0:T(512)S(1)} %bitcast.39, bf16[6,512,768]{2,1,0:T(8,128)(2,1)} %get-tuple-element.128, s32[]{:T(128)} %get-tuple-element.116), kind=kOutput, calls=%fused_computation.3.clone.1 | convolution fusion | flops 1210317312 | bytes 3160576 | tf_op jit(solution)/shard_map/while/body/eval_jaxpr/dot_general | solution.py:50
  161.9 3.3 %fusion.15 = f32[1536]{0:T(1024)S(1)} fusion(bf16[1536,768]{1,0:T(8,128)(2,1)} %get-tuple-element.129, s32[1536]{0:T(1024)S(1)} %get-tuple-element.127, s32[512]{0:T(512)S(1)} %bitcast.39, bf16[6,512,768]{2,1,0:T(8,128)(2,1)} %get-tuple-element.128, s32[]{:T(128)} %get-tuple-element.116), kind=kOutput, calls=%fused_computation.3.clone.1 | convolution fusion | flops 1210317312 | bytes 3160576 | tf_op jit(solution)/shard_map/while/body/eval_jaxpr/dot_general | solution.py:50
  166.0 3.3 %fusion.15 = f32[1536]{0:T(1024)S(1)} fusion(bf16[1536,768]{1,0:T(8,128)(2,1)} %get-tuple-element.129, s32[1536]{0:T(1024)S(1)} %get-tuple-element.127, s32[512]{0:T(512)S(1)} %bitcast.39, bf16[6,512,768]{2,1,0:T(8,128)(2,1)} %get-tuple-element.128, s32[]{:T(128)} %get-tuple-element.116), kind=kOutput, calls=%fused_computation.3.clone.1 | convolution fusion | flops 1210317312 | bytes 3160576 | tf_op jit(solution)/shard_map/while/body/eval_jaxpr/dot_general | solution.py:50
  170.1 3.3 %fusion.15 = f32[1536]{0:T(1024)S(1)} fusion(bf16[1536,768]{1,0:T(8,128)(2,1)} %get-tuple-element.129, s32[1536]{0:T(1024)S(1)} %get-tuple-element.127, s32[512]{0:T(512)S(1)} %bitcast.39, bf16[6,512,768]{2,1,0:T(8,128)(2,1)} %get-tuple-element.128, s32[]{:T(128)} %get-tuple-element.116), kind=kOutput, calls=%fused_computation.3.clone.1 | convolution fusion | flops 1210317312 | bytes 3160576 | tf_op jit(solution)/shard_map/while/body/eval_jaxpr/dot_general | solution.py:50
  173.5 6.4 %pmax.7 = f32[1536]{0:T(1024)S(1)} all-reduce(f32[1536]{0:T(1024)S(1)} %get-tuple-element.37), channel_id=1, replica_groups=mesh['row'=8,'col'=4] {'col'}, use_global_device_ids=true, to_apply=%region_4.5 | all-reduce | flops 1536 | bytes 12288 | tf_op jit(solution)/shard_map/pmax | solution.py:76
  (38 shorter events, 8.0 us)
Async XLA Ops:
  6.5 127.5 %copy-start = (bf16[384,768]{1,0:T(8,128)(2,1)S(1)}, bf16[384,768]{1,0:T(8,128)(2,1)}, u32[]{:S(2)}) copy-start(bf16[384,768]{1,0:T(8,128)(2,1)} %param.4) | copy-start | bytes 1769476
  6.5 142.3 %all-gather.4.cloned.1.call-start = ((), (), s32[]{:S(2)}) async-start(), calls=%async_computation | async-start | bytes 2949120 | tf_op jit(solution)/shard_map/all_gather | solution.py:66
  7.9 74.6 %copy-start.2 = (f32[384]{0:T(512)}, f32[384]{0:T(512)S(1)}, u32[]{:S(2)}) copy-start(f32[384]{0:T(512)S(1)} %add_rsqrt_fusion) | copy-start | bytes 4612
  9.1 19.4 %copy-start.1 = (bf16[384,768]{1,0:T(8,128)(2,1)}, bf16[384,768]{1,0:T(8,128)(2,1)S(1)}, u32[]{:S(2)}) copy-start(bf16[384,768]{1,0:T(8,128)(2,1)S(1)} %fusion.6) | copy-start | bytes 1769476
  9.1 19.4 %collective-permute-start = (bf16[384,768]{1,0:T(8,128)(2,1)S(1)}, bf16[384,768]{1,0:T(8,128)(2,1)S(1)}, u32[]{:S(2)}, u32[]{:S(2)}) collective-permute-start(bf16[384,768]{1,0:T(8,128)(2,1)S(1)} %fusion.6), channel_id=1, source_target_pairs={{0,4},{4,8},{8,12},{12,16},{16,20},{20,24},{24,28},{28,0},{1,5},{5... | collective-permute-start | bytes 1769480 | tf_op jit(solution)/shard_map/ppermute | solution.py:20
  28.5 24.9 %collective-permute-start.1 = (bf16[384,768]{1,0:T(8,128)(2,1)S(1)}, bf16[384,768]{1,0:T(8,128)(2,1)S(1)}, u32[]{:S(2)}, u32[]{:S(2)}) collective-permute-start(bf16[384,768]{1,0:T(8,128)(2,1)S(1)} %collective-permute-done), channel_id=1, source_target_pairs={{0,4},{4,8},{8,12},{12,16},{16,20},{20,24},{24,28},{28,0},{1,5},{5... | collective-permute-start | bytes 1769480 | tf_op jit(solution)/shard_map/ppermute | solution.py:20
  28.6 27.4 %collective-permute-start.4 = (bf16[384,768]{1,0:T(8,128)(2,1)}, bf16[384,768]{1,0:T(8,128)(2,1)S(1)}, u32[]{:S(2)}, u32[]{:S(2)}) collective-permute-start(bf16[384,768]{1,0:T(8,128)(2,1)} %copy-done.1), channel_id=1, source_target_pairs={{4,0},{8,4},{12,8},{16,12},{20,16},{24,20},{28,24},{0,28},{5,1},{9... | collective-permute-start | bytes 1769480 | tf_op jit(solution)/shard_map/ppermute | solution.py:22
  53.5 26.6 %collective-permute-start.2 = (bf16[384,768]{1,0:T(8,128)(2,1)S(1)}, bf16[384,768]{1,0:T(8,128)(2,1)S(1)}, u32[]{:S(2)}, u32[]{:S(2)}) collective-permute-start(bf16[384,768]{1,0:T(8,128)(2,1)S(1)} %collective-permute-done.1), channel_id=1, source_target_pairs={{0,4},{4,8},{8,12},{12,16},{16,20},{20,24},{24,28},{28,0},{1,5},{5... | collective-permute-start | bytes 1769480 | tf_op jit(solution)/shard_map/ppermute | solution.py:20
  56.0 70.7 %collective-permute-start.5 = (bf16[384,768]{1,0:T(8,128)(2,1)S(1)}, bf16[384,768]{1,0:T(8,128)(2,1)S(1)}, u32[]{:S(2)}, u32[]{:S(2)}) collective-permute-start(bf16[384,768]{1,0:T(8,128)(2,1)S(1)} %collective-permute-done.4), channel_id=1, source_target_pairs={{4,0},{8,4},{12,8},{16,12},{20,16},{24,20},{28,24},{0,28},{5,1},{9... | collective-permute-start | bytes 1769480 | tf_op jit(solution)/shard_map/ppermute | solution.py:22
  80.0 49.4 %collective-permute-start.3 = (bf16[384,768]{1,0:T(8,128)(2,1)S(1)}, bf16[384,768]{1,0:T(8,128)(2,1)}, u32[]{:S(2)}, u32[]{:S(2)}) collective-permute-start(bf16[384,768]{1,0:T(8,128)(2,1)S(1)} %collective-permute-done.2), channel_id=1, source_target_pairs={{0,4},{4,8},{8,12},{12,16},{16,20},{20,24},{24,28},{28,0},{1,5},{5... | collective-permute-start | bytes 1769480 | tf_op jit(solution)/shard_map/ppermute | solution.py:20
  126.7 7.4 %copy-start.3 = (f32[384]{0:T(512)S(1)}, f32[384]{0:T(512)}, u32[]{:S(2)}) copy-start(f32[384]{0:T(512)} %copy-done.2) | copy-start | bytes 4612
  126.7 15.9 %collective-permute-start.6 = (bf16[384,768]{1,0:T(8,128)(2,1)S(1)}, bf16[384,768]{1,0:T(8,128)(2,1)S(1)}, u32[]{:S(2)}, u32[]{:S(2)}) collective-permute-start(bf16[384,768]{1,0:T(8,128)(2,1)S(1)} %collective-permute-done.5), channel_id=1, source_target_pairs={{4,0},{8,4},{12,8},{16,12},{20,16},{24,20},{28,24},{0,28},{5,1},{9... | collective-permute-start | bytes 1769480 | tf_op jit(solution)/shard_map/ppermute | solution.py:22
  143.5 5.3 %copy-start.4 = (s32[1536]{0:T(1024)S(1)}, s32[1536]{0:T(1024)}, u32[]{:S(2)}) copy-start(s32[1536]{0:T(1024)} %reshape.71) | copy-start | bytes 18436
Sparse Core Ops, SparseCore 0:
  28.7 25.4 all-gather.3
